TPU v7x, 256 devices: a 4x2x16 block of a 4x16x16 slice. The times are simulated.
256 devices in a mesh: ga: 2 (over y), ea: 128 (over z, x, core).
Axes of the slice: x: 4, y: 2, z: 16, core: 2. Of those that a mesh axis runs over, the one named last changes fastest.
The devices are a block of a 4x16x16 slice.
Arguments:
- tokens: bfloat16 [32768, 2048], P(('ga', 'ea')), parts along dimension 0, may hold values from -6 to 6
- expert_choice_index: int32 [32768, 4], P(('ga', 'ea')), parts along dimension 0, may hold values from 0 to 63, all different within a row; in each aligned block of 128 rows (0 to 127, 128 to 255, ...) at most 9 rows name the same one
- router_gate_weight: float32 [32768, 4], P(('ga', 'ea')), parts along dimension 0, may hold values from 0.05 to 0.6
- cotangent: bfloat16 [32768, 2048], P(('ga', 'ea')), parts along dimension 0, may hold values from -6 to 6
- gate_up_matrix: bfloat16 [128, 2048, 1408], P('ea'), may hold values from -0.125 to 0.125
- down_weight: bfloat16 [128, 704, 2048], P('ea'), may hold values from -0.15625 to 0.15625
- adapter_input_projection: bfloat16 [2048, 16], replicated, may hold values from -0.125 to 0.125
- adapter_output_projection: bfloat16 [128, 16, 1408], P('ea'), may hold values from -0.59765625 to 0.59765625
Outputs:
- layer_output: bfloat16 [32768, 2048], P(('ga', 'ea')), parts along dimension 0
- adapter_input_gradient: float32 [4096, 16], P('ga'), parts along dimension 0
- lora_b_grad: float32 [256, 16, 1408], P(('ga', 'ea')), parts along dimension 0
There are 2 independent parts, one for each index of `ga`. A program takes and returns all parts, laid end to end along the dimension named above; an argument that names none is the same for every part. Nothing has to cross between parts.
Inputs may be any that keep to these rules, and one draw needn't show every extreme that they name: `expert_choice_index`: each row names 4 different experts. Within the rows of one device (aligned blocks of 128 rows) no expert is named by more than 9 rows, and in every draw some expert is named by exactly 9 rows of some block.
All inputs are finite; a program needn't handle non-finite values.
Results may differ from a plain program's by a relative error of at most 0.0072.
Values may be sent and summed in bfloat16 or wider, within the bound.
No kernel may reach another device: no remote copies, remote signals or barrier semaphores. Data moves between devices by JAX's collectives and lax.ppermute only.
A program may use at most 128 MiB of HBM per device.

v0:
```python
import jax
import jax.numpy as jnp
from jax import lax
from jax.sharding import Mesh
from jax.sharding import PartitionSpec as P

EXPERT_SPLIT = 2
EA = ("ea_0", "ea_1", "ea_2")
GA_EA = ("ga", "ea_0", "ea_1", "ea_2")
adapter_scale = 2.0


def from_partner(value, axis, distance):
    mask = 2**distance
    pairs = [(source, source ^ mask) for source in range(lax.axis_size(axis))]
    return lax.ppermute(value, axis, pairs)


def one_axis_at_a_time(array, axes):
    for axis in axes:
        array = lax.psum(array, axis)
    return array


def slot_ranks(id_block, experts):
    flat_ids = id_block.reshape(-1)
    onehot = (flat_ids[:, None] == jnp.arange(experts, dtype=jnp.int32)[None, :]).astype(jnp.int32)
    before = jnp.cumsum(onehot, axis=0) - onehot
    return jnp.sum(before * onehot, axis=1).reshape(id_block.shape)


def block_halfway(
    input_rows, output_gradient_rows, gate_up_weight, down_w, adapter_a, adapter_output_weight
):
    adapter_input_rows = jnp.dot(input_rows, adapter_a, preferred_element_type=jnp.float32).astype(
        jnp.bfloat16
    )
    joined_columns = jnp.dot(
        input_rows, gate_up_weight, preferred_element_type=jnp.float32
    ) + adapter_scale * jnp.dot(
        adapter_input_rows, adapter_output_weight, preferred_element_type=jnp.float32
    )
    block_width = down_w.shape[0]
    gate_part = joined_columns[:, :block_width]
    up_part = joined_columns[:, block_width:]
    sigmoid_gate = jax.nn.sigmoid(gate_part)
    active = gate_part * sigmoid_gate
    hidden = (active * up_part).astype(jnp.bfloat16)
    partial_value = jnp.dot(hidden, down_w, preferred_element_type=jnp.float32).astype(jnp.bfloat16)
    down_grad = lax.dot_general(
        output_gradient_rows, down_w, (((1,), (1,)), ((), ())), preferred_element_type=jnp.float32
    )
    gate_grad = down_grad * up_part * sigmoid_gate * (1.0 + gate_part * (1.0 - sigmoid_gate))
    up_grad = down_grad * active
    joined_gradient = jnp.concatenate([gate_grad, up_grad], axis=1).astype(jnp.bfloat16)
    output_gradient_part = adapter_scale * lax.dot_general(
        adapter_input_rows,
        joined_gradient,
        (((0,), (0,)), ((), ())),
        preferred_element_type=jnp.float32,
    )
    adapter_gradient = (
        adapter_scale
        * lax.dot_general(
            joined_gradient,
            adapter_output_weight,
            (((1,), (1,)), ((), ())),
            preferred_element_type=jnp.float32,
        )
    ).astype(jnp.bfloat16)
    grad_a = lax.dot_general(
        input_rows, adapter_gradient, (((0,), (0,)), ((), ())), preferred_element_type=jnp.float32
    )
    return (partial_value, grad_a, output_gradient_part)


def local(
    tokens,
    expert_choice_index,
    router_gate_weight,
    cotangent,
    gate_up_matrix,
    down_weight,
    adapter_input_projection,
    adapter_output_projection,
):
    devices = lax.axis_size(EA)
    experts = devices // EXPERT_SPLIT
    tok_rows, model_width = tokens.shape
    top_count = expert_choice_index.shape[1]
    capacity = 9 * tok_rows * top_count // (8 * experts)
    half_width = model_width // 2
    parity = lax.axis_index(EA) % 2
    slot_rank = slot_ranks(expert_choice_index, experts)
    slot_rows = (expert_choice_index * capacity + slot_rank).reshape(-1)
    scaled_dy = (router_gate_weight[:, :, None] * cotangent[:, None, :].astype(jnp.float32)).astype(
        jnp.bfloat16
    )
    repeated = jnp.broadcast_to(tokens[:, None, :], (tok_rows, top_count, model_width))
    both_rows = jnp.stack([repeated, scaled_dy], axis=2).reshape(
        tok_rows * top_count, 2, model_width
    )
    blank_rows = jnp.zeros((experts * capacity, 2, model_width), jnp.bfloat16)
    send_rows = blank_rows.at[slot_rows].set(both_rows, unique_indices=True)
    rows_total = devices * capacity
    halves = (
        send_rows.reshape(experts, capacity, 2, 2, half_width)
        .transpose(0, 3, 1, 2, 4)
        .reshape(devices, capacity, 2, half_width)
    )
    own_piece = lax.all_to_all(halves, EA, split_axis=0, concat_axis=0, tiled=True)
    other_piece = from_partner(own_piece, EA, 0)
    lower_block_part = jnp.where(parity == 0, own_piece, other_piece)
    upper_block_part = jnp.where(parity == 0, other_piece, own_piece)
    arrived = jnp.concatenate([lower_block_part, upper_block_part], axis=3)
    input_rows = arrived[:, :, 0].reshape(rows_total, model_width)
    output_gradient_rows = arrived[:, :, 1].reshape(rows_total, model_width)
    partial_value, input_gradient_local, output_gradient_part = block_halfway(
        input_rows,
        output_gradient_rows,
        gate_up_matrix[0],
        down_weight[0],
        adapter_input_projection,
        adapter_output_projection[0],
    )
    adapter_input_gradient = one_axis_at_a_time(input_gradient_local, EA)
    partial_value = partial_value.reshape(devices, capacity, model_width)
    kept_part = jnp.where(
        parity == 0, partial_value[:, :, :half_width], partial_value[:, :, half_width:]
    )
    given_part = jnp.where(
        parity == 0, partial_value[:, :, half_width:], partial_value[:, :, :half_width]
    )
    taken_part = from_partner(given_part, EA, 0)
    summed = (kept_part.astype(jnp.float32) + taken_part.astype(jnp.float32)).astype(jnp.bfloat16)
    returned = lax.all_to_all(summed, EA, split_axis=0, concat_axis=0, tiled=True)
    expert_out = (
        returned.reshape(experts, 2, capacity, half_width)
        .transpose(0, 2, 1, 3)
        .reshape(experts * capacity, model_width)
    )
    picked = expert_out[slot_rows].reshape(tok_rows, top_count, model_width).astype(jnp.float32)
    layer_output = jnp.sum(router_gate_weight[:, :, None] * picked, axis=1).astype(jnp.bfloat16)
    return (layer_output, adapter_input_gradient, output_gradient_part[None])


def solution(mesh):
    split = Mesh(mesh.devices.reshape(mesh.shape["ga"], 16, 4, 2), ("ga", "ea_0", "ea_1", "ea_2"))
    in_specs = (
        P(GA_EA, None),
        P(GA_EA, None),
        P(GA_EA, None),
        P(GA_EA, None),
        P(EA, None, None),
        P(EA, None, None),
        P(),
        P(EA, None, None),
    )
    out_specs = (P(GA_EA, None), P("ga", None), P(GA_EA, None, None))
    return jax.shard_map(local, mesh=split, in_specs=in_specs, out_specs=out_specs, check_vma=False)
```

profile of v0, /device:TPU:33, one launch (start us, length us, event | category | flops | bytes accessed | tf_op | source)
XLA Modules:
  0.0 807.9 jit_solution(12720040110281030694)
XLA Ops:
  12.0 4.2 mul.95
  16.2 5.3 mul.96
  23.9 4.0 stack_broadcast_in_dim.8
  33.0 8.5 %copy.75 = bf16[512,2,2048]{2,1,0:T(2,128)(2,1)} copy(bf16[512,2,2048]{2,0,1:T(8,128)(2,1)} %pad_maximum_fusion.1) | data formatting | bytes 8388608 | tf_op jit(solution)/shard_map/stack | solution.py:100
  41.5 4.6 broadcast_in_dim.4
  46.1 64.3 %scatter_fusion = bf16[576,2,2048]{2,1,0:T(2,128)(2,1)} fusion(bf16[576,2,2048]{2,1,0:T(2,128)(2,1)} %broadcast_in_dim.4, s32[512]{0:T(512)S(1)} %bitcast.57, bf16[512,2,2048]{2,1,0:T(2,128)(2,1)} %copy.75), kind=kCustom, calls=%fused_computation.1 | custom fusion | bytes 12584960 | tf_op jit(solution)/shard_map/scatter | solution.py:104
  110.4 13.7 %reshape.146 = bf16[64,9,2,2,1024]{4,3,2,1,0:T(2,128)(2,1)} reshape(bf16[576,2,2048]{2,1,0:T(2,128)(2,1)} %scatter_fusion) | data formatting | bytes 9437184 | tf_op jit(solution)/shard_map/reshape | solution.py:107
  124.0 8.3 %copy.77 = bf16[64,2,9,2,1024]{4,3,2,1,0:T(2,128)(2,1)} copy(bf16[64,2,9,2,1024]{4,1,3,2,0:T(2,128)(2,1)} %bitcast.54) | data formatting | bytes 9437184 | tf_op jit(solution)/shard_map/transpose | solution.py:108
  132.3 242.0 %all_to_all.10 = bf16[128,9,2,1024]{3,2,1,0:T(2,128)(2,1)} all-to-all(bf16[128,9,2,1024]{3,2,1,0:T(2,128)(2,1)} %bitcast.55), channel_id=1, replica_groups=mesh['ga'=2,'ea_0'=16,'ea_1'=4,'ea_2'=2] {'ea_0','ea_1','ea_2'}, dimensions={0} | all-to-all | bytes 9437184 | tf_op jit(solution)/shard_map/all_to_all | solution.py:111
  374.6 7.9 collective-permute-done
  382.6 10.9 %broadcast_select_fusion.1 = (bf16[128,9,2,1024]{3,2,1,0:T(2,128)(2,1)}, bf16[128,9,2,1024]{3,2,1,0:T(2,128)(2,1)}) fusion(bf16[128,9,2,1024]{3,2,1,0:T(2,128)(2,1)} %all_to_all.10, bf16[128,9,2,1024]{3,2,1,0:T(2,128)(2,1)} %collective-permute-done, pred[]{:T(512)S(6)} %eq.33), kind=kLoop, calls=%fused_computation.8 | loop fusion | flops 4718592 | bytes 18874368 | tf_op jit(solution)/shard_map/jit(_where)/select_n | solution.py:113
  393.5 65.1 %fusion.1 = (bf16[128,9,2048]{2,1,0:T(8,128)(2,1)}, bf16[128,9,2048]{2,1,0:T(8,128)(2,1)}) fusion(bf16[128,9,2,1024]{3,2,1,0:T(2,128)(2,1)} %get-tuple-element.8, bf16[128,9,2,1024]{3,2,1,0:T(2,128)(2,1)} %get-tuple-element.7), kind=kLoop, calls=%fused_computation.6 | loop fusion | flops 18874368 | bytes 18874368 | tf_op jit(solution)/shard_map/slice | solution.py:117
  458.5 8.5 %reshape_squeeze.6 = bf16[1152,2048]{1,0:T(8,128)(2,1)} reshape(bf16[128,9,2048]{2,1,0:T(8,128)(2,1)} %get-tuple-element.4) | data formatting | bytes 9437184 | tf_op jit(solution)/shard_map/reshape;squeeze | solution.py:116
  467.1 11.9 %fusion.2 = f32[1152,1408]{1,0:T(8,128)S(1)} fusion(bf16[1152,2048]{1,0:T(8,128)(2,1)} %reshape_squeeze.6, bf16[1,2048,1408]{2,1,0:T(8,128)(2,1)} %param.12), kind=kOutput, calls=%fused_computation.10 | convolution fusion | flops 6643777536 | bytes 16973824 | tf_op jit(solution)/shard_map/dot_general | solution.py:38
  484.1 5.6 convolution_convert_fusion
  489.8 8.1 %reshape.126 = bf16[128,9,2048]{2,1,0:T(8,128)(2,1)} reshape(bf16[1152,2048]{1,0:T(8,128)(2,1)} %convolution_convert_fusion) | data formatting | bytes 9437184 | tf_op jit(solution)/shard_map/reshape | solution.py:127
  497.9 3.9 fusion.25
  501.8 5.0 broadcast_select_fusion.2
  507.5 4.2 collective-permute-done.1
  511.7 3.7 add_convert_fusion
  515.4 3.6 copy.80
  519.0 9.9 %all-to-all-start.1 = ((bf16[128,9,1024]{2,1,0:T(8,128)(2,1)}), bf16[128,9,1024]{2,1,0:T(8,128)(2,1)}, u32[]{:S(2)}, u32[]{:S(2)}) async-start(bf16[128,9,1024]{2,1,0:T(8,128)(2,1)} %copy.80), calls=%async_computation.1 | async-start | bytes 8388608 | tf_op jit(solution)/shard_map/all_to_all | solution.py:136
  529.2 8.5 %reshape_squeeze.7 = bf16[1152,2048]{1,0:T(8,128)(2,1)} reshape(bf16[128,9,2048]{2,1,0:T(8,128)(2,1)} %get-tuple-element.3) | data formatting | bytes 9437184 | tf_op jit(solution)/shard_map/reshape;squeeze | solution.py:117
  537.7 11.1 %multiply_convert_fusion.2 = (bf16[1152,704]{1,0:T(8,128)(2,1)}, bf16[1152,704]{1,0:T(8,128)(2,1)}) fusion(f32[1152,1408]{1,0:T(8,128)} %copy-done.3, bf16[1152,2048]{1,0:T(8,128)(2,1)} %reshape_squeeze.7, bf16[1,704,2048]{2,1,0:T(8,128)(2,1)S(1)} %copy-done), kind=kOutput, calls=%fused_computation.17 | convolution fusion | flops 3332431872 | bytes 17334272 | tf_op jit(solution)/shard_map/dot_general | solution.py:50
  548.8 5.9 fusion.10
  554.8 145.5 %all-reduce.4.cloned.1.call-done = f32[2048,16]{0,1:T(8,128)} async-done(((f32[2048,16]{0,1:T(8,128)}), f32[2048,16]{0,1:T(8,128)}) %all-reduce.4.cloned.1.call-update) | async-done | bytes 131088 | tf_op jit(solution)/shard_map/psum | solution.py:21
  704.4 53.2 %all-reduce.6.cloned.1.call-done = f32[2048,16]{0,1:T(8,128)} async-done(((f32[2048,16]{0,1:T(8,128)}), f32[2048,16]{0,1:T(8,128)}) %all-reduce.6.cloned.1.call-update) | async-done | bytes 131088 | tf_op jit(solution)/shard_map/psum | solution.py:21
  757.6 4.9 copy.81
  764.6 7.2 gather_fusion
  771.8 4.8 reshape.129
  776.5 6.2 multiply_reduce_fusion
  782.8 16.8 %all-reduce.8.cloned.1.call-done = f32[2048,16]{0,1:T(8,128)} async-done(((f32[2048,16]{0,1:T(8,128)}), f32[2048,16]{0,1:T(8,128)}) %all-reduce.8.cloned.1.call-update) | async-done | bytes 131088 | tf_op jit(solution)/shard_map/psum | solution.py:21
  (49 shorter events, 26.6 us)
Async XLA Ops:
  7.2 477.0 %copy-start = (bf16[1,704,2048]{2,1,0:T(8,128)(2,1)S(1)}, bf16[1,704,2048]{2,1,0:T(8,128)(2,1)}, u32[]{:S(2)}) copy-start(bf16[1,704,2048]{2,1,0:T(8,128)(2,1)} %param.13) | copy-start | bytes 8650756
  16.2 5.3 copy-start.4
  27.9 2.9 copy-start.2
  374.3 8.3 %collective-permute-start = (bf16[128,9,2,1024]{3,2,1,0:T(2,128)(2,1)}, bf16[128,9,2,1024]{3,2,1,0:T(2,128)(2,1)}, u32[]{:S(2)}, u32[]{:S(2)}) collective-permute-start(bf16[128,9,2,1024]{3,2,1,0:T(2,128)(2,1)} %all_to_all.10), channel_id=1, source_target_pairs={{0,1},{1,0},{2,3},{3,2},{4,5},{5,4},{6,7},{7,6},{8,9},{9,8},{10,11... | collective-permute-start | bytes 14155784 | tf_op jit(solution)/shard_map/ppermute | solution.py:16
  467.1 11.9 %copy-start.1 = (bf16[1152,2048]{1,0:T(8,128)(2,1)S(1)}, bf16[1152,2048]{1,0:T(8,128)(2,1)}, u32[]{:S(2)}) copy-start(bf16[1152,2048]{1,0:T(8,128)(2,1)} %reshape_squeeze.6) | copy-start | bytes 14155780
  467.1 11.9 %copy-start.6 = (bf16[2048,16]{0,1:T(8,128)(2,1)S(1)}, bf16[2048,16]{0,1:T(8,128)(2,1)}, u32[]{:S(2)}) copy-start(bf16[2048,16]{0,1:T(8,128)(2,1)} %param.14) | copy-start | bytes 196612
  479.0 1.3 copy-start.5
  481.4 2.8 copy-start.3
  506.9 4.9 collective-permute-start.1
  519.0 238.6 %all-to-all-start.1 = ((bf16[128,9,1024]{2,1,0:T(8,128)(2,1)}), bf16[128,9,1024]{2,1,0:T(8,128)(2,1)}, u32[]{:S(2)}, u32[]{:S(2)}) async-start(bf16[128,9,1024]{2,1,0:T(8,128)(2,1)} %copy.80), calls=%async_computation.1 | async-start | bytes 8388608 | tf_op jit(solution)/shard_map/all_to_all | solution.py:136
  528.9 171.5 %all-reduce.4.cloned.1.call-start = ((), (), s32[]{:S(2)}) async-start(), calls=%async_computation.2 | async-start | bytes 262144 | tf_op jit(solution)/shard_map/psum | solution.py:21
  554.8 202.8 %all-reduce.6.cloned.1.call-start = ((), (), s32[]{:S(2)}) async-start(), calls=%async_computation.3 | async-start | bytes 262144 | tf_op jit(solution)/shard_map/psum | solution.py:21
  700.4 99.2 %all-reduce.8.cloned.1.call-start = ((), (), s32[]{:S(2)}) async-start(), calls=%async_computation.4 | async-start | bytes 262144 | tf_op jit(solution)/shard_map/psum | solution.py:21
Sparse Core Ops, SparseCore 0:
  554.9 145.3 all-reduce.3
  702.7 54.8 all-reduce.5
  760.1 39.4 all-reduce.7
where the time goes:
time: 819 us; the launch traced here: 808 us
  blocking collectives  242 us (30%)
  waiting for transfers between devices  228 us (28%)
  local copies, waits for them, and re-layouts  174 us (21%)
  other arithmetic  97.9 us (12%)
  matrix products  40.3 us (5%)
  between operations  14.1 us (2%)
  starting transfers between devices  11.7 us (1%)
    all_to_all x1, blocking collectives, local(): lax.all_to_all(halves, EA, split_axis=0, concat_axis=0, tiled=True)  242 us
    psum x3, waiting for transfers between devices, one_axis_at_a_time(): array = lax.psum(array, axis)  215 us
    slice x1, other arithmetic, local(): output_gradient_rows = arrived[:, :, 1].reshape(rows_total, model_width)  65.1 us
    scatter x1, local copies, waits for them, and re-layouts, local(): send_rows = blank_rows.at[slot_rows].set(both_rows, unique_indices=True)  64.3 us
  transfers between devices with their start and end apart: 6, of which 5 were waited for; matrix products, arithmetic and copies ran while one was open for 7% of the time, Pallas kernels for 0%

commit v1 on v0

--- a/solution.py
+++ b/solution.py
@@ -8,6 +8,7 @@
 EA = ("ea_0", "ea_1", "ea_2")
 GA_EA = ("ga", "ea_0", "ea_1", "ea_2")
 adapter_scale = 2.0
+derive_body = lambda tile_in, shard_axis: jnp.sum(lax.all_gather(tile_in, shard_axis), axis=0)
 
 
 def from_partner(value, axis, distance):
@@ -18,7 +19,7 @@
 
 def one_axis_at_a_time(array, axes):
     for axis in axes:
-        array = lax.psum(array, axis)
+        array = derive_body(array, axis)
     return array
 
 

time: 819 us -> 781 us (0.954)
  the two profiles are of different devices: /device:TPU:33 before, /device:TPU:40 now
where the time goes in v1:
time: 781 us; the launch traced here: 770 us
  blocking collectives  275 us (35%)
  local copies, waits for them, and re-layouts  177 us (23%)
  waiting for transfers between devices  150 us (19%)
  other arithmetic  100 us (13%)
  matrix products  40.4 us (5%)
  between operations  14.5 us (2%)
  starting transfers between devices  13.3 us (2%)
    all_to_all x1, blocking collectives, local(): lax.all_to_all(halves, EA, split_axis=0, concat_axis=0, tiled=True)  241 us
    all_gather x1, waiting for transfers between devices, lax.all_gather(tile_in, shard_axis)  124 us
    slice x1, other arithmetic, local(): output_gradient_rows = arrived[:, :, 1].reshape(rows_total, model_width)  65.1 us
    scatter x1, local copies, waits for them, and re-layouts, local(): send_rows = blank_rows.at[slot_rows].set(both_rows, unique_indices=True)  64.2 us
    all_gather x2, blocking collectives, lax.all_gather(tile_in, shard_axis)  34.1 us
  transfers between devices with their start and end apart: 4, of which 4 were waited for; matrix products, arithmetic and copies ran while one was open for 5% of the time, Pallas kernels for 0%

profile of v1, /device:TPU:40, one launch (start us, length us, event | category | flops | bytes accessed | tf_op | source)
XLA Modules:
  0.0 770.3 jit_solution(14020321876487825296)
XLA Ops:
  12.0 4.2 mul.95
  16.2 5.3 mul.96
  23.9 4.0 stack_broadcast_in_dim.8
  33.0 8.5 %copy.90 = bf16[512,2,2048]{2,1,0:T(2,128)(2,1)} copy(bf16[512,2,2048]{2,0,1:T(8,128)(2,1)} %pad_maximum_fusion.1) | data formatting | bytes 8388608 | tf_op jit(solution)/shard_map/stack | solution.py:101
  41.5 4.6 broadcast_in_dim.4
  46.1 64.2 %scatter_fusion = bf16[576,2,2048]{2,1,0:T(2,128)(2,1)} fusion(bf16[576,2,2048]{2,1,0:T(2,128)(2,1)} %broadcast_in_dim.4, s32[512]{0:T(512)S(1)} %bitcast.67, bf16[512,2,2048]{2,1,0:T(2,128)(2,1)} %copy.90), kind=kCustom, calls=%fused_computation.1 | custom fusion | bytes 12584960 | tf_op jit(solution)/shard_map/scatter | solution.py:105
  110.3 13.9 %reshape.149 = bf16[64,9,2,2,1024]{4,3,2,1,0:T(2,128)(2,1)} reshape(bf16[576,2,2048]{2,1,0:T(2,128)(2,1)} %scatter_fusion) | data formatting | bytes 9437184 | tf_op jit(solution)/shard_map/reshape | solution.py:108
  124.2 8.3 %copy.92 = bf16[64,2,9,2,1024]{4,3,2,1,0:T(2,128)(2,1)} copy(bf16[64,2,9,2,1024]{4,1,3,2,0:T(2,128)(2,1)} %bitcast.63) | data formatting | bytes 9437184 | tf_op jit(solution)/shard_map/transpose | solution.py:109
  132.5 240.9 %all_to_all.10 = bf16[128,9,2,1024]{3,2,1,0:T(2,128)(2,1)} all-to-all(bf16[128,9,2,1024]{3,2,1,0:T(2,128)(2,1)} %bitcast.64), channel_id=1, replica_groups=mesh['ga'=2,'ea_0'=16,'ea_1'=4,'ea_2'=2] {'ea_0','ea_1','ea_2'}, dimensions={0} | all-to-all | bytes 9437184 | tf_op jit(solution)/shard_map/all_to_all | solution.py:112
  373.6 8.0 %collective-permute-done = bf16[128,9,2,1024]{3,2,1,0:T(2,128)(2,1)} collective-permute-done((bf16[128,9,2,1024]{3,2,1,0:T(2,128)(2,1)}, bf16[128,9,2,1024]{3,2,1,0:T(2,128)(2,1)}, u32[]{:S(2)}, u32[]{:S(2)}) %collective-permute-start) | collective-permute-done | bytes 4718624 | tf_op jit(solution)/shard_map/ppermute | solution.py:17
  381.7 10.6 %broadcast_select_fusion.1 = (bf16[128,9,2,1024]{3,2,1,0:T(2,128)(2,1)}, bf16[128,9,2,1024]{3,2,1,0:T(2,128)(2,1)}) fusion(bf16[128,9,2,1024]{3,2,1,0:T(2,128)(2,1)} %all_to_all.10, bf16[128,9,2,1024]{3,2,1,0:T(2,128)(2,1)} %collective-permute-done, pred[]{:T(512)S(6)} %eq.33), kind=kLoop, calls=%fused_computation.8 | loop fusion | flops 4718592 | bytes 18874368 | tf_op jit(solution)/shard_map/jit(_where)/select_n | solution.py:114
  392.3 65.1 %fusion.1 = (bf16[128,9,2048]{2,1,0:T(8,128)(2,1)}, bf16[128,9,2048]{2,1,0:T(8,128)(2,1)}) fusion(bf16[128,9,2,1024]{3,2,1,0:T(2,128)(2,1)} %get-tuple-element.8, bf16[128,9,2,1024]{3,2,1,0:T(2,128)(2,1)} %get-tuple-element.7), kind=kLoop, calls=%fused_computation.6 | loop fusion | flops 18874368 | bytes 18874368 | tf_op jit(solution)/shard_map/slice | solution.py:118
  457.4 8.5 %reshape_squeeze.6 = bf16[1152,2048]{1,0:T(8,128)(2,1)} reshape(bf16[128,9,2048]{2,1,0:T(8,128)(2,1)} %get-tuple-element.4) | data formatting | bytes 9437184 | tf_op jit(solution)/shard_map/reshape;squeeze | solution.py:117
  465.9 11.9 %fusion.2 = f32[1152,1408]{1,0:T(8,128)S(1)} fusion(bf16[1152,2048]{1,0:T(8,128)(2,1)} %reshape_squeeze.6, bf16[1,2048,1408]{2,1,0:T(8,128)(2,1)} %param.12), kind=kOutput, calls=%fused_computation.10 | convolution fusion | flops 6643777536 | bytes 16973824 | tf_op jit(solution)/shard_map/dot_general | solution.py:39
  483.0 5.6 convolution_convert_fusion
  488.6 8.0 %reshape.126 = bf16[128,9,2048]{2,1,0:T(8,128)(2,1)} reshape(bf16[1152,2048]{1,0:T(8,128)(2,1)} %convolution_convert_fusion) | data formatting | bytes 9437184 | tf_op jit(solution)/shard_map/reshape | solution.py:128
  496.7 3.9 fusion.25
  500.6 5.0 broadcast_select_fusion.2
  506.4 4.3 collective-permute-done.1
  510.7 3.7 add_convert_fusion
  514.4 3.5 copy.95
  517.9 12.2 %all-to-all-start.1 = ((bf16[128,9,1024]{2,1,0:T(8,128)(2,1)}), bf16[128,9,1024]{2,1,0:T(8,128)(2,1)}, u32[]{:S(2)}, u32[]{:S(2)}) async-start(bf16[128,9,1024]{2,1,0:T(8,128)(2,1)} %copy.95), calls=%async_computation.1 | async-start | bytes 8388608 | tf_op jit(solution)/shard_map/all_to_all | solution.py:137
  530.3 8.5 %reshape_squeeze.7 = bf16[1152,2048]{1,0:T(8,128)(2,1)} reshape(bf16[128,9,2048]{2,1,0:T(8,128)(2,1)} %get-tuple-element.3) | data formatting | bytes 9437184 | tf_op jit(solution)/shard_map/reshape;squeeze | solution.py:118
  538.8 11.1 %multiply_convert_fusion.2 = (bf16[1152,704]{1,0:T(8,128)(2,1)}, bf16[1152,704]{1,0:T(8,128)(2,1)}) fusion(f32[1152,1408]{1,0:T(8,128)} %copy-done.3, bf16[1152,2048]{1,0:T(8,128)(2,1)} %reshape_squeeze.7, bf16[1,704,2048]{2,1,0:T(8,128)(2,1)S(1)} %copy-done), kind=kOutput, calls=%fused_computation.17 | convolution fusion | flops 3332431872 | bytes 17334272 | tf_op jit(solution)/shard_map/dot_general | solution.py:51
  549.9 5.9 fusion.10
  559.4 124.2 %all-gather.5.cloned.1.call-done = f32[32768,16]{0,1:T(8,128)} async-done(((f32[2048,16]{0,1:T(8,128)}), f32[32768,16]{0,1:T(8,128)}) %all-gather.5.cloned.1.call-update) | async-done | bytes 2097168 | tf_op jit(solution)/shard_map/all_gather | solution.py:11
  686.8 31.9 %all-gather.1 = f32[8192,16]{0,1:T(8,128)S(1)} all-gather(f32[2048,16]{0,1:T(8,128)S(1)} %bitcast_reduce_fusion), channel_id=3, replica_groups=mesh['ga'=2,'ea_0'=16,'ea_1'=4,'ea_2'=2] {'ea_1'}, dimensions={0}, use_global_device_ids=true | all-gather | bytes 655360 | tf_op jit(solution)/shard_map/all_gather | solution.py:11
  724.6 13.3 %all-to-all-done.1 = bf16[128,9,1024]{2,1,0:T(8,128)(2,1)} async-done(((bf16[128,9,1024]{2,1,0:T(8,128)(2,1)}), bf16[128,9,1024]{2,1,0:T(8,128)(2,1)}, u32[]{:S(2)}, u32[]{:S(2)}) %all-to-all-start.1) | async-done | bytes 2359328 | tf_op jit(solution)/shard_map/all_to_all | solution.py:137
  738.0 4.9 copy.96
  744.9 7.3 gather_fusion
  752.2 4.8 reshape.129
  757.0 6.2 multiply_reduce_fusion
  (50 shorter events, 33.4 us)
Async XLA Ops:
  7.2 475.8 %copy-start = (bf16[1,704,2048]{2,1,0:T(8,128)(2,1)S(1)}, bf16[1,704,2048]{2,1,0:T(8,128)(2,1)}, u32[]{:S(2)}) copy-start(bf16[1,704,2048]{2,1,0:T(8,128)(2,1)} %param.13) | copy-start | bytes 8650756
  16.2 5.3 copy-start.4
  27.9 2.9 copy-start.2
  373.4 8.3 %collective-permute-start = (bf16[128,9,2,1024]{3,2,1,0:T(2,128)(2,1)}, bf16[128,9,2,1024]{3,2,1,0:T(2,128)(2,1)}, u32[]{:S(2)}, u32[]{:S(2)}) collective-permute-start(bf16[128,9,2,1024]{3,2,1,0:T(2,128)(2,1)} %all_to_all.10), channel_id=1, source_target_pairs={{0,1},{1,0},{2,3},{3,2},{4,5},{5,4},{6,7},{7,6},{8,9},{9,8},{10,11... | collective-permute-start | bytes 14155784 | tf_op jit(solution)/shard_map/ppermute | solution.py:17
  465.9 11.9 %copy-start.1 = (bf16[1152,2048]{1,0:T(8,128)(2,1)S(1)}, bf16[1152,2048]{1,0:T(8,128)(2,1)}, u32[]{:S(2)}) copy-start(bf16[1152,2048]{1,0:T(8,128)(2,1)} %reshape_squeeze.6) | copy-start | bytes 14155780
  465.9 11.9 %copy-start.6 = (bf16[2048,16]{0,1:T(8,128)(2,1)S(1)}, bf16[2048,16]{0,1:T(8,128)(2,1)}, u32[]{:S(2)}) copy-start(bf16[2048,16]{0,1:T(8,128)(2,1)} %param.14) | copy-start | bytes 196612
  477.8 1.3 copy-start.5
  480.2 2.8 copy-start.3
  505.6 5.1 collective-permute-start.1
  517.9 220.0 %all-to-all-start.1 = ((bf16[128,9,1024]{2,1,0:T(8,128)(2,1)}), bf16[128,9,1024]{2,1,0:T(8,128)(2,1)}, u32[]{:S(2)}, u32[]{:S(2)}) async-start(bf16[128,9,1024]{2,1,0:T(8,128)(2,1)} %copy.95), calls=%async_computation.1 | async-start | bytes 8388608 | tf_op jit(solution)/shard_map/all_to_all | solution.py:137
  530.1 153.5 %all-gather.5.cloned.1.call-start = ((), (), s32[]{:S(2)}) async-start(), calls=%async_computation.2 | async-start | bytes 2228224 | tf_op jit(solution)/shard_map/all_gather | solution.py:11
Sparse Core Ops, SparseCore 0:
  556.0 127.5 all-gather.4
